TPU v7x, 32 devices: a whole 2x2x4 slice. The times are simulated.
32 devices in a mesh: dp: 4 (over y, x), cls: 8 (over z, core).
Axes of the slice: x: 2, y: 2, z: 4, core: 2. Of those that a mesh axis runs over, the one named last changes fastest.
Arguments:
- sketches: bfloat16 [8192, 4096], P(('dp', 'cls')), may hold values from -6 to 6
- labels: int32 [8192], P(('dp', 'cls')), may hold values from 0 to 7, as said below
- places: int32 [8192], P(('dp', 'cls')), may hold values from 0 to 2047, as said below
- counts: int32 [8, 4, 32], P('cls'), may hold values from 0 to 16, as said below
- chosen: int32 [3, 8], P(None, 'cls'), may hold values from 0 to 2047, as said below
Outputs:
- gain_scores: float32 [3, 8, 2048], P(None, 'cls', 'dp')
- coverage: float32 [8, 2048], P('cls', 'dp')
Inputs may be any that keep to these rules, and one draw needn't show every extreme that they name: `labels`: every class has 4 or more examples. `places`: an example of device s (its index along dp and cls together) with class k has place m * 512 + s * 16 + j in class k's block: m is the member of dp that receives it, and for each k, m and s the j run over 0 to counts[k, m, s] - 1 without gaps, so no two examples share a place. In every draw one class and member receive 16 examples from every device. counts[k, m, s] is the number of examples of device s that take places of class k on member m. chosen[t, k] is a place of class k's block that holds an example; the 3 picks of a class differ.
All inputs are finite; a program needn't handle non-finite values.
Results may differ from a plain program's by a relative error of at most 0.0003.
Values may be sent and summed in bfloat16 or wider, within the bound.
A program may use at most 128 MiB of HBM per device.

v0:
```python
import functools

import jax
import jax.numpy as jnp
from jax import lax
from jax.experimental import pallas as pl
from jax.experimental.pallas import tpu as pltpu
from jax.sharding import PartitionSpec as P

MESH = pl.DeviceIdType.MESH


def ring_place(index):
    high = index // 2
    return 2 * high + (index % 2 + high) % 2


def ring_member(place):
    high = place // 2
    return 2 * high + (place % 2 + high) % 2


def exchange_kernel(
    members,
    owners,
    out_ref,
    table_ref,
    inner_ref,
    pick_inner_ref,
    norms_ref,
    pick_norms_ref,
    rows_ref,
    picks_ref,
    a_send,
    a_recv,
    own_sem,
    b_send,
    b_recv,
    p_send,
    p_recv,
):
    member = lax.axis_index("dp")
    owner = lax.axis_index("cls")
    chunks, unit, width = out_ref.shape[1:]
    capacity = chunks * owners * unit
    group = min(chunks, max(1, 256 // (owners * unit)))
    span = group * owners * unit
    half = members // 2
    place = ring_place(member)
    side = owner % 2
    step = 1 - 2 * side
    contract = (((1,), (1,)), ((), ()))

    barrier = pltpu.get_barrier_semaphore()
    for hop in range(1, owners):
        pl.semaphore_signal(
            barrier, inc=1, device_id=(member, (owner + hop) % owners), device_id_type=MESH
        )
    for hop in range(1, members):
        pl.semaphore_signal(
            barrier,
            inc=1,
            device_id=(ring_member((place + hop) % members), owner),
            device_id_type=MESH,
        )
    pl.semaphore_wait(barrier, owners + members - 2)

    mine = pl.ds(pl.multiple_of(owner * unit, unit), unit)

    def dispatch(chunk, hop):
        target = (owner + hop) % owners
        return pltpu.make_async_remote_copy(
            src_ref=out_ref.at[target, chunk],
            dst_ref=rows_ref.at[0, chunk, mine],
            send_sem=a_send.at[chunk, hop - 1],
            recv_sem=a_recv.at[chunk, hop - 1],
            device_id=(member, target),
            device_id_type=MESH,
        )

    def own_copy(chunk):
        return pltpu.make_async_copy(
            out_ref.at[owner, chunk], rows_ref.at[0, chunk, mine], own_sem.at[chunk]
        )

    def share(chunk, hop):
        target = ring_member((place + step * hop + members) % members)
        return pltpu.make_async_remote_copy(
            src_ref=rows_ref.at[0, chunk],
            dst_ref=rows_ref.at[hop, chunk],
            send_sem=b_send.at[chunk, hop - 1],
            recv_sem=b_recv.at[chunk, hop - 1],
            device_id=(target, owner),
            device_id_type=MESH,
        )

    def share_picks(hop):
        return pltpu.make_async_remote_copy(
            src_ref=picks_ref.at[0],
            dst_ref=picks_ref.at[hop],
            send_sem=p_send.at[hop - 1],
            recv_sem=p_recv.at[hop - 1],
            device_id=(ring_member((place + hop) % members), owner),
            device_id_type=MESH,
        )

    def own_rows():
        return rows_ref[0].reshape(capacity, width)

    def multiply(slot, first):
        block = rows_ref[slot, first : first + group].reshape(span, width)
        low = slot * capacity + first * owners * unit
        inner_ref[:, low : low + span] = lax.dot_general(
            own_rows(), block, contract, preferred_element_type=jnp.float32
        )
        wide = block.astype(jnp.float32)
        norms_ref[low : low + span, :] = jnp.sum(wide * wide, axis=1, keepdims=True)

    sends_half = (place // half + side) % 2 == 0
    gets_half = (place // half + side) % 2 == 1

    for chunk in range(chunks):
        own_copy(chunk).start()
        for hop in range(1, owners):
            dispatch(chunk, hop).start()
    for chunk in range(chunks):
        own_copy(chunk).wait()
        for hop in range(1, owners):
            dispatch(chunk, hop).wait_recv()

        @pl.when(sends_half)
        def _(chunk=chunk):
            share(chunk, half).start()

        for hop in range(1, half):
            share(chunk, hop).start()

    picks_ref[0] = lax.dot_general(
        table_ref[...],
        own_rows(),
        (((1,), (0,)), ((), ())),
        preferred_element_type=jnp.float32,
    ).astype(picks_ref.dtype)
    for first in range(0, chunks, group):
        multiply(0, first)
    for hop in range(1, members):
        share_picks(hop).start()

    for first in range(0, chunks, group):
        for hop in range(1, half):
            for chunk in range(first, first + group):
                share(chunk, hop).wait_recv()
            multiply(hop, first)

        @pl.when(gets_half)
        def _(first=first):
            for chunk in range(first, first + group):
                share(chunk, half).wait_recv()
            multiply(half, first)

    for hop in range(1, members):
        share_picks(hop).wait_recv()
    picks = picks_ref[0].astype(jnp.float32)
    for hop in range(1, members):
        picks = picks + picks_ref[hop].astype(jnp.float32)
    pick_norms_ref[...] = jnp.sum(picks * picks, axis=1, keepdims=True)
    picks = picks.astype(picks_ref.dtype)

    def multiply_picks(slot):
        pick_inner_ref[:, slot * capacity : (slot + 1) * capacity] = lax.dot_general(
            picks,
            rows_ref[slot].reshape(capacity, width),
            contract,
            preferred_element_type=jnp.float32,
        )

    for slot in range(half):
        multiply_picks(slot)

    @pl.when(gets_half)
    def _():
        multiply_picks(half)

    for chunk in range(chunks):
        for hop in range(1, owners):
            dispatch(chunk, hop).wait_send()
        for hop in range(1, half):
            share(chunk, hop).wait_send()

        @pl.when(sends_half)
        def _(chunk=chunk):
            share(chunk, half).wait_send()

    for hop in range(1, members):
        share_picks(hop).wait_send()


def exchange(outgoing, pick_table, members, owners):
    chunks, unit, width = outgoing.shape[1:]
    capacity = chunks * owners * unit
    padded = pick_table.shape[0]
    slots = members // 2 + 1
    vmem = pl.BlockSpec(memory_space=pltpu.VMEM)
    return pl.pallas_call(
        functools.partial(exchange_kernel, members, owners),
        out_shape=(
            jax.ShapeDtypeStruct((capacity, slots * capacity), jnp.float32),
            jax.ShapeDtypeStruct((padded, slots * capacity), jnp.float32),
            jax.ShapeDtypeStruct((slots * capacity, 1), jnp.float32),
            jax.ShapeDtypeStruct((padded, 1), jnp.float32),
        ),
        in_specs=[vmem, vmem],
        out_specs=(vmem, vmem, vmem, vmem),
        scratch_shapes=[
            pltpu.VMEM((slots, chunks, owners * unit, width), outgoing.dtype),
            pltpu.VMEM((members, padded, width), outgoing.dtype),
            pltpu.SemaphoreType.DMA((chunks, owners - 1)),
            pltpu.SemaphoreType.DMA((chunks, owners - 1)),
            pltpu.SemaphoreType.DMA((chunks,)),
            pltpu.SemaphoreType.DMA((chunks, members // 2)),
            pltpu.SemaphoreType.DMA((chunks, members // 2)),
            pltpu.SemaphoreType.DMA((members - 1,)),
            pltpu.SemaphoreType.DMA((members - 1,)),
        ],
        compiler_params=pltpu.CompilerParams(
            collective_id=0, has_side_effects=True, vmem_limit_bytes=60 * 1024 * 1024
        ),
    )(outgoing, pick_table)


def body(sketches, labels, places, counts, chosen):
    row_count, width = sketches.shape
    members = lax.axis_size("dp")
    owners = lax.axis_size("cls")
    devices = members * owners
    sub = 2 * row_count // devices
    capacity = devices * sub
    unit = 16
    chunks = members * sub // unit
    half = members // 2
    slots = half + 1
    member = lax.axis_index("dp")
    owner = lax.axis_index("cls")
    picked = chosen[:, 0]
    pick_count = picked.shape[0]

    target = (labels * members + places // capacity) * sub + places % sub
    send_table = (
        lax.broadcasted_iota(jnp.int32, (2 * row_count, row_count), 0) == target[None, :]
    ).astype(jnp.bfloat16)
    outgoing = jnp.dot(send_table, sketches, preferred_element_type=jnp.float32).astype(
        jnp.bfloat16
    )
    step = 1 - 2 * (owner % 2)
    place = ring_place(member)
    slot_member = jnp.stack(
        [ring_member((place - step * hop + members) % members) for hop in range(slots)]
    )
    has_half = (place // half + owner % 2) % 2 == 1
    slot_here = (jnp.arange(slots) < half) | has_half

    class_counts = counts[0]
    valid_places = (
        lax.broadcasted_iota(jnp.int32, (members, devices, sub), 2) < class_counts[:, :, None]
    )
    valid_blocks = jnp.transpose(
        jnp.transpose(valid_places.reshape(members, members, owners, sub), (1, 2, 0, 3)).reshape(
            members, owners, chunks, unit
        ),
        (0, 2, 1, 3),
    ).reshape(members, capacity)
    slot_valid = (
        jnp.stack([lax.dynamic_index_in_dim(valid_blocks, slot_member[s], 0, False) for s in range(slots)])
        & slot_here[:, None]
    )
    column_valid = slot_valid.reshape(-1)
    own_valid = slot_valid[0]
    total = jnp.sum(class_counts).astype(jnp.float32)

    source = picked % capacity // sub
    offset = picked // capacity * sub + picked % sub
    pick_index = (offset // unit * owners + source % owners) * unit + offset % unit
    pick_table = (
        (jnp.arange(capacity)[None, :] == pick_index[:, None])
        & (source // owners == member)[:, None]
    ).astype(jnp.bfloat16)
    pick_table = jnp.pad(pick_table, ((0, -pick_count % 16), (0, 0)))

    inner, pick_inner, norms, pick_norms = exchange(
        outgoing.reshape(owners, chunks, unit, width), pick_table, members, owners
    )
    norms = norms[:, 0]
    spread = (norms[:capacity, None] + norms[None, :] - 2.0 * inner) / width
    pick_spread = (
        pick_norms[:pick_count] + norms[None, :] - 2.0 * pick_inner[:pick_count]
    ) / width

    largest = jnp.max(
        jnp.where(own_valid[:, None] & column_valid[None, :], spread, 0.0)
    )
    bound = jnp.max(
        lax.all_to_all(
            jnp.broadcast_to(largest, (members, 1, 128)), "dp", split_axis=0, concat_axis=0, tiled=True
        )
    )

    pick_similar = bound - pick_spread
    current = jnp.zeros((slots * capacity,), jnp.float32)
    column_gain = []
    row_gain = []
    similar = bound - spread
    far = similar[:, capacity:]
    for turn in range(pick_count):
        near_cover = current[:capacity]
        column_gain.append(
            jnp.sum(
                jnp.where(
                    own_valid[:, None] & column_valid[None, :],
                    jnp.maximum(similar - near_cover[:, None], 0.0),
                    0.0,
                ),
                axis=0,
            )
        )
        row_gain.append(
            jnp.sum(
                jnp.where(
                    column_valid[None, capacity:],
                    jnp.maximum(far - current[None, capacity:], 0.0),
                    0.0,
                ),
                axis=1,
            )
        )
        current = jnp.maximum(current, pick_similar[turn])
    column_gain = jnp.stack(column_gain).reshape(pick_count, slots, capacity)
    near_gain = column_gain[:, 0] + jnp.stack(row_gain)
    own_cover = current[:capacity]

    near = jnp.concatenate([near_gain, own_cover[None]], axis=0)
    held = jnp.concatenate(
        [
            near[:, None],
            jnp.concatenate(
                [column_gain[:, 1:], jnp.zeros((1, slots - 1, capacity), jnp.float32)], axis=0
            ),
        ],
        axis=1,
    )
    spots = jnp.arange(members)[:, None] == slot_member[None, :]
    spots = spots & slot_here[None, :]
    placed = jnp.sum(jnp.where(spots[None, :, :, None], held[:, None], 0.0), axis=2)
    placed = jnp.transpose(
        placed.reshape(pick_count + 1, members, chunks, owners, unit), (0, 1, 3, 2, 4)
    ).reshape(pick_count + 1, members, owners, members, sub)
    placed = jnp.transpose(placed, (3, 0, 1, 2, 4)).reshape(members, pick_count + 1, capacity)
    summed = jnp.sum(
        lax.all_to_all(placed, "dp", split_axis=0, concat_axis=0, tiled=True), axis=0
    )
    place_valid = lax.dynamic_index_in_dim(
        valid_places.reshape(members, capacity), member, 0, keepdims=False
    ).astype(jnp.float32)
    gain_scores = (summed[:pick_count] * place_valid[None, :] / total)[:, None, :]
    coverage = (summed[pick_count] * place_valid)[None, :]
    return (gain_scores, coverage)


def solution(mesh):
    placed = (
        P(("dp", "cls"), None),
        P(("dp", "cls")),
        P(("dp", "cls")),
        P("cls", None, None),
        P(None, "cls"),
    )
    return jax.shard_map(
        body,
        mesh=mesh,
        in_specs=placed,
        out_specs=(P(None, "cls", "dp"), P("cls", "dp")),
        check_vma=False,
    )
```

profile of v0, /device:TPU:8, one launch (start us, length us, event | category | flops | bytes accessed | tf_op | source)
XLA Modules:
  0.0 198.0 jit_solution(2393860486764117409)
XLA Ops:
  0.9 0.9 lt.143
  1.8 0.1 lt.145
  1.9 0.1 lt.146
  2.0 0.1 iota.47
  2.3 0.7 compare_bitcast_fusion
  2.9 0.7 fusion.14
  3.6 0.1 fusion.8
  3.7 0.6 pad_convert_fusion.table_ref
  4.3 0.7 fusion.10
  5.0 3.2 %convolution_convert_fusion = bf16[512,4096]{1,0:T(8,128)(2,1)} fusion(bf16[256,4096]{1,0:T(8,128)(2,1)S(1)} %copy-done, s32[256]{0:T(256)S(1)} %fusion.10), kind=kOutput, calls=%fused_computation | convolution fusion | flops 1075970048 | bytes 6292480 | tf_op jit(solution)/shard_map/dot_general | solution.py:251
  8.2 151.3 %shard_map.68 = (f32[512,1536]{1,0:T(8,128)}, f32[16,1536]{1,0:T(8,128)}, f32[1536,1]{1,0:T(8,128)}, f32[16,1]{1,0:T(8,128)}) custom-call(bf16[8,4,16,4096]{3,2,1,0:T(8,128)(2,1)} %bitcast.31, bf16[16,512]{1,0:T(8,128)(2,1)} %pad_convert_fusion.table_ref), custom_call_target="tpu_custom_call" | custom-call | tf_op jit(solution)/shard_map/pallas_call | solution.py:204
  159.5 1.1 slice_reduce_fusion
  160.6 1.4 reduce.3
  162.1 3.4 %fusion = f32[]{:T(128)} fusion(f32[512,1536]{1,0:T(8,128)} %get-tuple-element.7, f32[1536]{0:T(1024)S(1)} %reduce.3, f32[512]{0:T(512)S(1)} %slice_reduce_fusion, pred[1536]{0:T(1024)(128)(4,1)S(1)} %and.233, pred[512]{0:T(512)(128)(4,1)S(1)} %slice_reduce_fusion.1), kind=kLoop, calls=%fused_computation.5 | loop fusion | flops 5505023 | bytes 3155972 | tf_op jit(solution)/shard_map/reduce_max | solution.py:298
  165.5 1.1 broadcast_in_dim.83
  166.6 6.3 %all-to-all-start = ((f32[4,1,128]{2,1,0:T(1,128)}), f32[4,1,128]{2,1,0:T(1,128)S(1)}, u32[]{:S(2)}, u32[]{:S(2)}) async-start(f32[4,1,128]{2,1,0:T(1,128)} %broadcast_in_dim.83), calls=%async_computation | async-start | bytes 4096 | tf_op jit(solution)/shard_map/all_to_all | solution.py:302
  173.1 0.8 slice_reduce_fusion.2
  173.9 0.1 iota.51
  174.1 0.1 lt.158
  174.2 3.4 %all-to-all-done = f32[4,1,128]{2,1,0:T(1,128)S(1)} async-done(((f32[4,1,128]{2,1,0:T(1,128)}), f32[4,1,128]{2,1,0:T(1,128)S(1)}, u32[]{:S(2)}, u32[]{:S(2)}) %all-to-all-start) | async-done | bytes 2080 | tf_op jit(solution)/shard_map/all_to_all | solution.py:302
  177.6 0.6 reduce_max.19
  178.2 1.5 multiply_subtract_fusion
  179.7 5.4 %fusion.3 = (f32[1536]{0:T(1024)S(1)}, f32[1536]{0:T(1024)S(1)}, f32[1536]{0:T(1024)S(1)}, f32[512,1536]{1,0:T(8,128)}) fusion(f32[512]{0:T(512)S(1)} %bitcast.41, pred[1536]{0:T(1024)(128)(4,1)S(1)} %and.233, pred[512]{0:T(512)(128)(4,1)S(1)} %slice_reduce_fusion.1, f32[512]{0:T(512)S(1)} %bitcast.40, f32[512,1536]{1,0:T(8,128)} %get-tuple-element.7, ...), kind=kLoop, calls=%fused_computation.8 | loop fusion | flops 13364736 | bytes 6324228 | tf_op jit(solution)/shard_map/reduce_sum | solution.py:316
  185.2 2.5 %select_reduce_fusion.2 = (f32[512]{0:T(512)S(1)}, f32[512]{0:T(512)S(1)}, f32[512]{0:T(512)S(1)}) fusion(f32[512,1536]{1,0:T(8,128)} %get-tuple-element.24, pred[1024]{0:T(1024)(128)(4,1)S(1)} %broadcast_in_dim.85, f32[1024]{0:T(1024)S(1)} %bitcast.35, f32[1024]{0:T(1024)S(1)} %bitcast.36), kind=kLoop, calls=%fused_computation.13 | loop fusion | flops 5765632 | bytes 2112512 | tf_op jit(solution)/shard_map/reduce_sum | solution.py:326
  187.8 0.1 select_reduce_fusion.3
  187.9 0.1 reshape.115
  188.1 0.8 reshape.116
  188.8 3.3 %all-to-all-start.1 = ((f32[4,4,512]{2,1,0:T(4,128)}), f32[4,4,512]{2,1,0:T(4,128)S(1)}, u32[]{:S(2)}, u32[]{:S(2)}) async-start(f32[4,4,512]{2,1,0:T(4,128)} %reshape.116), calls=%async_computation.1 | async-start | bytes 65536 | tf_op jit(solution)/shard_map/all_to_all | solution.py:358
  192.1 0.6 reduce_sum.89
  193.4 3.4 %all-to-all-done.1 = f32[4,4,512]{2,1,0:T(4,128)S(1)} async-done(((f32[4,4,512]{2,1,0:T(4,128)}), f32[4,4,512]{2,1,0:T(4,128)S(1)}, u32[]{:S(2)}, u32[]{:S(2)}) %all-to-all-start.1) | async-done | bytes 32800 | tf_op jit(solution)/shard_map/all_to_all | solution.py:358
  196.8 0.6 compare_select_fusion
  197.4 0.6 copy.24
  (39 shorter events, 0.6 us)
Async XLA Ops:
  0.6 4.4 %copy-start = (bf16[256,4096]{1,0:T(8,128)(2,1)S(1)}, bf16[256,4096]{1,0:T(8,128)(2,1)}, u32[]{:S(2)}) copy-start(bf16[256,4096]{1,0:T(8,128)(2,1)} %param.5) | copy-start | bytes 6291460
  159.5 14.5 %copy-start.1 = (s32[1,4,32]{2,1,0:T(4,128)S(1)}, s32[1,4,32]{2,1,0:T(4,128)}, u32[]{:S(2)}) copy-start(s32[1,4,32]{2,1,0:T(4,128)} %param.8) | copy-start | bytes 1540
  166.6 10.9 %all-to-all-start = ((f32[4,1,128]{2,1,0:T(1,128)}), f32[4,1,128]{2,1,0:T(1,128)S(1)}, u32[]{:S(2)}, u32[]{:S(2)}) async-start(f32[4,1,128]{2,1,0:T(1,128)} %broadcast_in_dim.83), calls=%async_computation | async-start | bytes 4096 | tf_op jit(solution)/shard_map/all_to_all | solution.py:302
  188.8 8.0 %all-to-all-start.1 = ((f32[4,4,512]{2,1,0:T(4,128)}), f32[4,4,512]{2,1,0:T(4,128)S(1)}, u32[]{:S(2)}, u32[]{:S(2)}) async-start(f32[4,4,512]{2,1,0:T(4,128)} %reshape.116), calls=%async_computation.1 | async-start | bytes 65536 | tf_op jit(solution)/shard_map/all_to_all | solution.py:358
where the time goes:
time: 199 us; the launch traced here: 198 us
  Pallas kernels  151 us (76%)
  other arithmetic  19.3 us (10%)
  starting transfers between devices  9.58 us (5%)
  waiting for transfers between devices  6.77 us (3%)
  local copies, waits for them, and re-layouts  6.17 us (3%)
  matrix products  3.18 us (2%)
    pallas_call x1, Pallas kernels, exchange(): pl.pallas_call(functools.partial(exchange_kernel, members, owners), out_s...  151 us
    all_to_all x1, starting transfers between devices, body(): lax.all_to_all(jnp.broadcast_to(largest, (members, 1, 128)), 'dp', split_...  6.32 us
    reduce_sum x1, other arithmetic, body(): jnp.sum(jnp.where(own_valid[:, None] & column_valid[None, :], jnp.maximum...  5.4 us
  transfers between devices with their start and end apart: 2, of which 2 were waited for; matrix products, arithmetic and copies ran while one was open for 1% of the time, Pallas kernels for 0%

commit v1 on v0

v1 whole, which is shorter than its diff:
```python
import functools

import jax
import jax.numpy as jnp
from jax import lax
from jax.experimental import pallas as pl
from jax.experimental.pallas import tpu as pltpu
from jax.sharding import PartitionSpec as P

MESH = pl.DeviceIdType.MESH
UNIT = 16
PICK_ROWS = 16
PARTS = 8
WINDOW = 3
FAR = 1e30


def ring_place(index):
    high = index // 2
    return 2 * high + (index % 2 + high) % 2


def ring_member(place):
    high = place // 2
    return 2 * high + (place % 2 + high) % 2


def dot_rows(left, right):
    return lax.dot_general(
        left, right, (((1,), (1,)), ((), ())), preferred_element_type=jnp.float32
    )


def class_kernel(
    members,
    owners,
    sub,
    steps,
    target_ref,
    pick_ref,
    counts_ref,
    sketch_ref,
    result_ref,
    table_ref,
    out_ref,
    rows_ref,
    picks_ref,
    inner_ref,
    pick_inner_ref,
    squares_ref,
    pick_squares_ref,
    bound_ref,
    wide_ref,
    row_gain_ref,
    gains_ref,
    final_ref,
    a_send,
    a_recv,
    b_send,
    b_recv,
    p_send,
    p_recv,
    m_send,
    m_recv,
    g_send,
    g_recv,
):
    member = lax.axis_index("dp")
    owner = lax.axis_index("cls")
    row_count, width = sketch_ref.shape
    parts, part = out_ref.shape[0], out_ref.shape[-1]
    chunks = rows_ref.shape[2]
    lanes = owners * UNIT
    capacity = chunks * lanes
    half = members // 2
    slots = half + 1
    window = min(WINDOW, parts - 1)
    place = ring_place(member)
    step = 1 - 2 * (owner % 2)
    sends_half = (place // half + owner % 2) % 2 == 0
    gets_half = (place // half + owner % 2) % 2 == 1
    scale = 1.0 / width

    barrier = pltpu.get_barrier_semaphore()
    for hop in range(1, owners):
        pl.semaphore_signal(
            barrier, inc=1, device_id=(member, (owner + hop) % owners), device_id_type=MESH
        )
    for hop in range(1, members):
        pl.semaphore_signal(
            barrier,
            inc=1,
            device_id=(ring_member((place + hop) % members), owner),
            device_id_type=MESH,
        )

    def dispatch(f, hop):
        target = (owner + hop) % owners
        return pltpu.make_async_remote_copy(
            src_ref=out_ref.at[f, target],
            dst_ref=rows_ref.at[0, f, :, owner],
            send_sem=a_send.at[f, hop - 1],
            recv_sem=a_recv.at[f, hop - 1],
            device_id=(member, target),
            device_id_type=MESH,
        )

    def share(f, hop):
        target = ring_member((place + step * hop + members) % members)
        return pltpu.make_async_remote_copy(
            src_ref=rows_ref.at[0, f],
            dst_ref=rows_ref.at[hop, f],
            send_sem=b_send.at[f, hop - 1],
            recv_sem=b_recv.at[f, hop - 1],
            device_id=(target, owner),
            device_id_type=MESH,
        )

    def share_picks(f, hop):
        return pltpu.make_async_remote_copy(
            src_ref=picks_ref.at[0, f],
            dst_ref=picks_ref.at[hop, f],
            send_sem=p_send.at[f, hop - 1],
            recv_sem=p_recv.at[f, hop - 1],
            device_id=(ring_member((place + hop) % members), owner),
            device_id_type=MESH,
        )

    def share_bound(hop):
        return pltpu.make_async_remote_copy(
            src_ref=bound_ref.at[0],
            dst_ref=bound_ref.at[hop],
            send_sem=m_send.at[hop - 1],
            recv_sem=m_recv.at[hop - 1],
            device_id=(ring_member((place + hop) % members), owner),
            device_id_type=MESH,
        )

    def share_gains(hop):
        target = ring_member((place + hop) % members)
        return pltpu.make_async_remote_copy(
            src_ref=gains_ref.at[target * sub // UNIT],
            dst_ref=final_ref.at[members - hop],
            send_sem=g_send.at[hop - 1],
            recv_sem=g_recv.at[hop - 1],
            device_id=(target, owner),
            device_id_type=MESH,
        )

    def prepare(f):
        low = pl.multiple_of(f * part, part)
        block = jnp.dot(
            table_ref[...],
            sketch_ref[:, pl.ds(low, part)],
            preferred_element_type=jnp.float32,
        ).astype(out_ref.dtype)
        out_ref[f] = block.reshape(out_ref.shape[1:])
        rows_ref[0, f, :, owner] = out_ref[f, owner]

    def part_rows(slot, f):
        return rows_ref[slot, f].reshape(capacity, part)

    def multiply(slot, f):
        block = part_rows(slot, f)
        product = dot_rows(part_rows(0, f), block)
        for chunk in range(chunks):
            inner_ref[slot * chunks + chunk] += product[:, chunk * lanes : (chunk + 1) * lanes]
        total = jnp.zeros((capacity, 128), jnp.float32)
        for low in range(0, part, 128):
            wide = block[:, low : low + 128].astype(jnp.float32)
            total = total + wide * wide
        squares_ref[slot] += total

    def multiply_picks(slot, f, picks):
        pick_inner_ref[slot] += dot_rows(picks, part_rows(slot, f))

    def own_part(f):
        picks_ref[0, f] = lax.dot_general(
            pick_table,
            part_rows(0, f),
            (((1,), (0,)), ((), ())),
            preferred_element_type=jnp.float32,
        ).astype(picks_ref.dtype)
        multiply(0, f)
        for hop in range(1, members):
            share_picks(f, hop).start()

    def other_part(f):
        for hop in range(1, members):
            share_picks(f, hop).wait_recv()
        picks = picks_ref[0, f].astype(jnp.float32)
        for hop in range(1, members):
            picks = picks + picks_ref[hop, f].astype(jnp.float32)
        total = jnp.zeros((PICK_ROWS, 128), jnp.float32)
        for low in range(0, part, 128):
            wide = picks[:, low : low + 128]
            total = total + wide * wide
        pick_squares_ref[...] += total
        picks = picks.astype(picks_ref.dtype)
        multiply_picks(0, f, picks)
        for hop in range(1, half):
            share(f, hop).wait_recv()
            multiply(hop, f)
            multiply_picks(hop, f, picks)

        @pl.when(gets_half)
        def _():
            share(f, half).wait_recv()
            multiply(half, f)
            multiply_picks(half, f, picks)

    table_ref[...] = (
        lax.broadcasted_iota(jnp.int32, (2 * row_count, row_count), 0) == target_ref[...]
    ).astype(table_ref.dtype)
    for f in range(window + 1):
        prepare(f)
    pl.semaphore_wait(barrier, owners + members - 2)
    for f in range(window):
        for hop in range(1, owners):
            dispatch(f, hop).start()

    inner_ref[...] = jnp.zeros_like(inner_ref)
    pick_inner_ref[...] = jnp.zeros_like(pick_inner_ref)
    squares_ref[...] = jnp.zeros_like(squares_ref)
    pick_squares_ref[...] = jnp.zeros_like(pick_squares_ref)
    pick_table = (
        lax.broadcasted_iota(jnp.int32, (PICK_ROWS, capacity), 1) + member * capacity
        == pick_ref[:, :1]
    ).astype(rows_ref.dtype)

    @pl.loop(0, parts)
    def _(f):
        for hop in range(1, owners):
            dispatch(f, hop).wait_recv()

        @pl.when(sends_half)
        def _():
            share(f, half).start()

        for hop in range(1, half):
            share(f, hop).start()

        @pl.when(f + window < parts)
        def _():
            for hop in range(1, owners):
                dispatch(f + window, hop).start()

        @pl.when(f + window + 1 < parts)
        def _():
            prepare(f + window + 1)

        own_part(f)

        @pl.when(f > 0)
        def _():
            other_part(f - 1)

    other_part(parts - 1)

    lane = lax.broadcasted_iota(jnp.int32, (members * owners, lanes), 1)
    source = lax.broadcasted_iota(jnp.int32, (members * owners, lanes), 0)
    spot = lax.broadcasted_iota(jnp.int32, (1, lanes), 1) & (sub - 1)
    lows = UNIT // sub
    unit_bits = UNIT.bit_length() - 1
    sub_bits = sub.bit_length() - 1

    def valid_row(slot):
        block = ring_member((place - step * slot + members) % members)
        filled = jnp.zeros((chunks, lanes), jnp.float32)
        for low in range(lows):
            spread_out = (source == block * owners + (lane >> unit_bits)) & (
                ((lane >> sub_bits) & (lows - 1)) == low
            )
            filled = filled + jnp.dot(
                counts_ref[low].astype(jnp.float32).astype(jnp.bfloat16),
                spread_out.astype(jnp.bfloat16),
                preferred_element_type=jnp.float32,
            )
        row = filled > spot.astype(jnp.float32)
        if slot == half:
            row = row & gets_half
        row = row.astype(jnp.float32)
        return jnp.concatenate([row[chunk : chunk + 1] for chunk in range(chunks)], axis=1)

    def turned(row):
        return jnp.transpose(jnp.broadcast_to(row, (128, capacity)))

    valid = [valid_row(slot) > 0.5 for slot in range(slots)]
    norm = [
        jnp.sum(jnp.transpose(squares_ref[slot]), axis=0, keepdims=True) * scale
        for slot in range(slots)
    ]
    pick_norm = jnp.sum(pick_squares_ref[...], axis=1, keepdims=True) * scale

    wide_ref[0] = turned(jnp.where(valid[0], norm[0], -FAR))
    near = wide_ref[0]
    if lanes > 128:
        near = jnp.concatenate([near] * (lanes // 128), axis=1)
    largest = jnp.zeros((1, lanes), jnp.float32)
    for slot in range(slots):
        for chunk in range(chunks):
            cut = slice(chunk * lanes, (chunk + 1) * lanes)
            tile = jnp.max(
                near - (2.0 * scale) * inner_ref[slot * chunks + chunk], axis=0, keepdims=True
            )
            tile = jnp.where(valid[slot][:, cut], tile + norm[slot][:, cut], 0.0)
            largest = jnp.maximum(largest, tile)
    bound_ref[0] = jnp.broadcast_to(jnp.max(largest, axis=1, keepdims=True), bound_ref.shape[1:])
    for hop in range(1, members):
        share_bound(hop).start()
    for hop in range(1, members):
        share_bound(hop).wait_recv()
    bound = bound_ref[0]
    for hop in range(1, members):
        bound = jnp.maximum(bound, bound_ref[hop])
    bound = bound[:1, :1]

    covers = []
    for slot in range(slots):
        cover = jnp.zeros((1, capacity), jnp.float32)
        held = [cover]
        for turn in range(steps):
            similar = bound - (
                pick_norm[turn : turn + 1]
                + norm[slot]
                - (2.0 * scale) * pick_inner_ref[slot][turn : turn + 1]
            )
            cover = jnp.maximum(cover, similar)
            held.append(cover)
        covers.append(held)

    for turn in range(steps):
        wide_ref[turn] = turned(
            jnp.where(valid[0], bound - norm[0] - covers[0][turn], -FAR)
        )
    row_gain_ref[...] = jnp.zeros_like(row_gain_ref)
    open_near = turned(bound - norm[0])
    wide_ref[steps] = open_near

    def repeat(block):
        if lanes > 128:
            block = jnp.concatenate([block] * (lanes // 128), axis=1)
        return block

    for slot in range(slots):
        for chunk in range(chunks):
            cut = slice(chunk * lanes, (chunk + 1) * lanes)
            tile = (2.0 * scale) * inner_ref[slot * chunks + chunk] - norm[slot][:, cut]
            gained = []
            for turn in range(steps):
                gained.append(
                    jnp.sum(
                        jnp.maximum(tile + repeat(wide_ref[turn]), 0.0), axis=0, keepdims=True
                    )
                )
                if slot > 0:
                    far = jnp.where(valid[slot][:, cut], covers[slot][turn][:, cut], FAR)
                    each = jnp.maximum(tile + repeat(wide_ref[steps]) - far, 0.0)
                    for low in range(0, lanes, 128):
                        row_gain_ref[turn] += each[:, low : low + 128]
            if slot == half:
                gained = [jnp.where(gets_half, row, 0.0) for row in gained]
            last = covers[0][steps][:, cut] if slot == 0 else jnp.zeros((1, lanes), jnp.float32)
            blank = jnp.zeros((8 - steps - 1, lanes), jnp.float32)
            gains_ref[chunk, slot] = jnp.concatenate([*gained, last, blank], axis=0)
    for turn in range(steps):
        row = jnp.sum(jnp.transpose(row_gain_ref[turn]), axis=0, keepdims=True)
        for chunk in range(chunks):
            gains_ref[chunk, 0, turn : turn + 1] += row[:, chunk * lanes : (chunk + 1) * lanes]

    for hop in range(1, members):
        share_gains(hop).start()
    final_ref[0] = gains_ref[member * sub // UNIT]
    for hop in range(1, members):
        share_gains(hop).wait_recv()
    for ahead in range(members):
        summed = final_ref[ahead, 0]
        for slot in range(1, slots):
            summed = summed + final_ref[(ahead + step * slot + members) % members, slot]
        block = ring_member((place + ahead) % members)
        result_ref[:, pl.ds(pl.multiple_of(block * lanes, lanes), lanes)] = summed

    @pl.loop(0, parts)
    def _(f):
        for hop in range(1, owners):
            dispatch(f, hop).wait_send()
        for hop in range(1, half):
            share(f, hop).wait_send()
        for hop in range(1, members):
            share_picks(f, hop).wait_send()

        @pl.when(sends_half)
        def _():
            share(f, half).wait_send()

    for hop in range(1, members):
        share_bound(hop).wait_send()
        share_gains(hop).wait_send()


def class_gains(target, picks, counts, sketches, members, owners, sub, steps):
    row_count, width = sketches.shape
    chunks = members * sub // UNIT
    lanes = owners * UNIT
    capacity = chunks * lanes
    slots = members // 2 + 1
    part = width // PARTS
    kind = sketches.dtype
    vmem = pl.BlockSpec(memory_space=pltpu.VMEM)
    dma = pltpu.SemaphoreType.DMA
    return pl.pallas_call(
        functools.partial(class_kernel, members, owners, sub, steps),
        out_shape=jax.ShapeDtypeStruct((8, members * lanes), jnp.float32),
        in_specs=[vmem, vmem, vmem, vmem],
        out_specs=vmem,
        scratch_shapes=[
            pltpu.VMEM((2 * row_count, row_count), kind),
            pltpu.VMEM((PARTS, owners, chunks, UNIT, part), kind),
            pltpu.VMEM((slots, PARTS, chunks, owners, UNIT, part), kind),
            pltpu.VMEM((members, PARTS, PICK_ROWS, part), kind),
            pltpu.VMEM((slots * chunks, capacity, lanes), jnp.float32),
            pltpu.VMEM((slots, PICK_ROWS, capacity), jnp.float32),
            pltpu.VMEM((slots, capacity, 128), jnp.float32),
            pltpu.VMEM((PICK_ROWS, 128), jnp.float32),
            pltpu.VMEM((members, 8, 128), jnp.float32),
            pltpu.VMEM((steps + 1, capacity, 128), jnp.float32),
            pltpu.VMEM((steps, capacity, 128), jnp.float32),
            pltpu.VMEM((chunks, slots, 8, lanes), jnp.float32),
            pltpu.VMEM((members, slots, 8, lanes), jnp.float32),
            dma((PARTS, owners - 1)),
            dma((PARTS, owners - 1)),
            dma((PARTS, members // 2)),
            dma((PARTS, members // 2)),
            dma((PARTS, members - 1)),
            dma((PARTS, members - 1)),
            dma((members - 1,)),
            dma((members - 1,)),
            dma((members - 1,)),
            dma((members - 1,)),
        ],
        compiler_params=pltpu.CompilerParams(
            collective_id=0, has_side_effects=True, vmem_limit_bytes=60 * 1024 * 1024
        ),
    )(target, picks, counts, sketches)


def body(sketches, labels, places, counts, chosen):
    row_count = sketches.shape[0]
    members = lax.axis_size("dp")
    owners = lax.axis_size("cls")
    devices = members * owners
    sub = 2 * row_count // devices
    capacity = devices * sub
    chunks = members * sub // UNIT
    lows = UNIT // sub
    member = lax.axis_index("dp")
    steps = chosen.shape[0]

    target = (labels * members + places // capacity) * sub + places % sub
    source = chosen % capacity // sub
    offset = chosen // capacity * sub + chosen % sub
    pick = (offset // UNIT * owners + source % owners) * UNIT + offset % UNIT
    pick = jnp.pad(
        source // owners * capacity + pick, ((0, PICK_ROWS - steps), (0, 127)), constant_values=-1
    )
    class_counts = counts[0]
    filled = jnp.transpose(class_counts.reshape(chunks, lows, devices), (1, 0, 2))

    result = class_gains(
        target.reshape(1, row_count), pick, filled, sketches, members, owners, sub, steps
    )
    total = jnp.sum(class_counts).astype(jnp.float32)
    if lows > 1:
        result = lax.dynamic_index_in_dim(
            result.reshape(8, members * owners, lows, sub), member % lows, 2, False
        ).reshape(8, capacity)
    mine = lax.dynamic_index_in_dim(class_counts, member, 0, False)
    spot = lax.broadcasted_iota(jnp.int32, (devices, sub), 1)
    place_valid = (spot < mine[:, None]).reshape(capacity).astype(jnp.float32)
    gain_scores = (result[:steps] * place_valid[None, :] / total)[:, None, :]
    coverage = (result[steps] * place_valid)[None, :]
    return (gain_scores, coverage)


def solution(mesh):
    placed = (
        P(("dp", "cls"), None),
        P(("dp", "cls")),
        P(("dp", "cls")),
        P("cls", None, None),
        P(None, "cls"),
    )
    return jax.shard_map(
        body,
        mesh=mesh,
        in_specs=placed,
        out_specs=(P(None, "cls", "dp"), P("cls", "dp")),
        check_vma=False,
    )
```

time: 199 us -> 151 us (0.76)
  the two profiles are of different devices: /device:TPU:8 before, /device:TPU:24 now
where the time goes in v1:
time: 151 us; the launch traced here: 150 us
  Pallas kernels  142 us (94%)
  other arithmetic  4.04 us (3%)
  local copies, waits for them, and re-layouts  2.86 us (2%)
    pallas_call x1, Pallas kernels, class_gains(): pl.pallas_call(functools.partial(class_kernel, members, owners, sub, step...  142 us

profile of v1, /device:TPU:24, one launch (start us, length us, event | category | flops | bytes accessed | tf_op | source)
XLA Modules:
  0.0 150.5 jit_solution(12312675987972378779)
XLA Ops:
  0.6 0.0 copy-start
  0.6 0.7 dynamic-slice_bitcast_fusion
  1.4 0.1 iota_compare_fusion
  1.5 0.1 reshape.43
  1.5 0.7 copy.12
  2.3 0.6 pad.4.pick_ref
  2.9 1.3 fusion.16
  4.2 142.2 %shard_map.68 = f32[8,512]{1,0:T(8,128)} custom-call(s32[1,256]{1,0:T(1,128)} %bitcast.5, s32[16,128]{1,0:T(8,128)} %pad.4.pick_ref, s32[1,4,32]{2,1,0:T(4,128)} %counts_ref.1, bf16[256,4096]{1,0:T(8,128)(2,1)} %sketch_ref.1), custom_call_target="tpu_custom_call" | custom-call | tf_op jit(solution)/shard_map/pallas_call | solution.py:411
  146.4 0.0 copy-done
  146.4 0.6 reduce_sum.9
  147.7 0.7 divide_bitcast_fusion
  148.5 0.6 copy.16
  149.1 0.1 lt.62
  149.2 1.3 slice_select_fusion
  (1 shorter events, 0.0 us)
Async XLA Ops:
  0.6 145.8 %copy-start = (s32[1,4,32]{2,1,0:T(4,128)S(1)}, s32[1,4,32]{2,1,0:T(4,128)}, u32[]{:S(2)}) copy-start(s32[1,4,32]{2,1,0:T(4,128)} %counts_ref.1) | copy-start | bytes 1540

commit v2 on v1

--- a/solution.py
+++ b/solution.py
@@ -11,7 +11,7 @@
 UNIT = 16
 PICK_ROWS = 16
 PARTS = 8
-WINDOW = 3
+WINDOW = 2
 FAR = 1e30
 
 
@@ -58,6 +58,8 @@
     a_recv,
     b_send,
     b_recv,
+    x_send,
+    x_recv,
     p_send,
     p_recv,
     m_send,
@@ -77,8 +79,12 @@
     window = min(WINDOW, parts - 1)
     place = ring_place(member)
     step = 1 - 2 * (owner % 2)
-    sends_half = (place // half + owner % 2) % 2 == 0
-    gets_half = (place // half + owner % 2) % 2 == 1
+    ring = (step * place + members) % members
+    cut_chunk = chunks // 2
+    gets_first = ring < half
+    gets_second = (ring >= 1) & (ring <= half)
+    gives_first = (ring + 1) % members < half
+    gives_second = ring >= half
     scale = 1.0 / width
 
     barrier = pltpu.get_barrier_semaphore()
@@ -112,6 +118,27 @@
             dst_ref=rows_ref.at[hop, f],
             send_sem=b_send.at[f, hop - 1],
             recv_sem=b_recv.at[f, hop - 1],
+            device_id=(target, owner),
+            device_id_type=MESH,
+        )
+
+    def share_first(f):
+        return pltpu.make_async_remote_copy(
+            src_ref=rows_ref.at[half - 1, f, :cut_chunk],
+            dst_ref=rows_ref.at[half, f, :cut_chunk],
+            send_sem=x_send.at[f, 0],
+            recv_sem=x_recv.at[f, 0],
+            device_id=(ring_member((place + step + members) % members), owner),
+            device_id_type=MESH,
+        )
+
+    def share_second(f):
+        target = ring_member((place + step * (half + 1) + members * half) % members)
+        return pltpu.make_async_remote_copy(
+            src_ref=rows_ref.at[0, f, cut_chunk:],
+            dst_ref=rows_ref.at[half, f, cut_chunk:],
+            send_sem=x_send.at[f, 1],
+            recv_sem=x_recv.at[f, 1],
             device_id=(target, owner),
             device_id_type=MESH,
         )
@@ -160,19 +187,23 @@
     def part_rows(slot, f):
         return rows_ref[slot, f].reshape(capacity, part)
 
-    def multiply(slot, f):
-        block = part_rows(slot, f)
-        product = dot_rows(part_rows(0, f), block)
-        for chunk in range(chunks):
-            inner_ref[slot * chunks + chunk] += product[:, chunk * lanes : (chunk + 1) * lanes]
-        total = jnp.zeros((capacity, 128), jnp.float32)
-        for low in range(0, part, 128):
-            wide = block[:, low : low + 128].astype(jnp.float32)
+    def multiply(slot, f, left=0, first=0, last=chunks):
+        low, high = first * lanes, last * lanes
+        block = rows_ref[slot, f, first:last].reshape(high - low, part)
+        product = dot_rows(part_rows(left, f), block)
+        for chunk in range(first, last):
+            cut = slice(chunk * lanes - low, (chunk + 1) * lanes - low)
+            inner_ref[slot * chunks + chunk] += product[:, cut]
+        total = jnp.zeros((high - low, 128), jnp.float32)
+        for spot in range(0, part, 128):
+            wide = block[:, spot : spot + 128].astype(jnp.float32)
             total = total + wide * wide
-        squares_ref[slot] += total
-
-    def multiply_picks(slot, f, picks):
-        pick_inner_ref[slot] += dot_rows(picks, part_rows(slot, f))
+        squares_ref[slot, low:high] += total
+
+    def multiply_picks(slot, f, picks, first=0, last=chunks):
+        low, high = first * lanes, last * lanes
+        block = rows_ref[slot, f, first:last].reshape(high - low, part)
+        pick_inner_ref[slot, :, low:high] += dot_rows(picks, block)
 
     def own_part(f):
         picks_ref[0, f] = lax.dot_general(
@@ -186,6 +217,13 @@
             share_picks(f, hop).start()
 
     def other_part(f):
+        for hop in range(1, half):
+            share(f, hop).wait_recv()
+
+        @pl.when(gives_first)
+        def _():
+            share_first(f).start()
+
         for hop in range(1, members):
             share_picks(f, hop).wait_recv()
         picks = picks_ref[0, f].astype(jnp.float32)
@@ -199,15 +237,20 @@
         picks = picks.astype(picks_ref.dtype)
         multiply_picks(0, f, picks)
         for hop in range(1, half):
-            share(f, hop).wait_recv()
             multiply(hop, f)
             multiply_picks(hop, f, picks)
 
-        @pl.when(gets_half)
-        def _():
-            share(f, half).wait_recv()
-            multiply(half, f)
-            multiply_picks(half, f, picks)
+        @pl.when(gets_second)
+        def _():
+            share_second(f).wait_recv()
+            multiply(half, f, 1, cut_chunk, chunks)
+            multiply_picks(half, f, picks, cut_chunk, chunks)
+
+        @pl.when(gets_first)
+        def _():
+            share_first(f).wait_recv()
+            multiply(half, f, 0, 0, cut_chunk)
+            multiply_picks(half, f, picks, 0, cut_chunk)
 
     table_ref[...] = (
         lax.broadcasted_iota(jnp.int32, (2 * row_count, row_count), 0) == target_ref[...]
@@ -233,12 +276,12 @@
         for hop in range(1, owners):
             dispatch(f, hop).wait_recv()
 
-        @pl.when(sends_half)
-        def _():
-            share(f, half).start()
-
         for hop in range(1, half):
             share(f, hop).start()
+
+        @pl.when(gives_second)
+        def _():
+            share_second(f).start()
 
         @pl.when(f + window < parts)
         def _():
@@ -264,8 +307,8 @@
     unit_bits = UNIT.bit_length() - 1
     sub_bits = sub.bit_length() - 1
 
-    def valid_row(slot):
-        block = ring_member((place - step * slot + members) % members)
+    def block_row(behind):
+        block = ring_member((place - step * behind + members * half) % members)
         filled = jnp.zeros((chunks, lanes), jnp.float32)
         for low in range(lows):
             spread_out = (source == block * owners + (lane >> unit_bits)) & (
@@ -276,11 +319,16 @@
                 spread_out.astype(jnp.bfloat16),
                 preferred_element_type=jnp.float32,
             )
-        row = filled > spot.astype(jnp.float32)
-        if slot == half:
-            row = row & gets_half
-        row = row.astype(jnp.float32)
+        row = (filled > spot.astype(jnp.float32)).astype(jnp.float32)
         return jnp.concatenate([row[chunk : chunk + 1] for chunk in range(chunks)], axis=1)
+
+    def valid_row(slot):
+        if slot < half:
+            return block_row(slot)
+        split = cut_chunk * lanes
+        first = jnp.where(gets_first, block_row(half)[:, :split], 0.0)
+        second = jnp.where(gets_second, block_row(half + 1)[:, split:], 0.0)
+        return jnp.concatenate([first, second], axis=1)
 
     def turned(row):
         return jnp.transpose(jnp.broadcast_to(row, (128, capacity)))
@@ -292,14 +340,21 @@
     ]
     pick_norm = jnp.sum(pick_squares_ref[...], axis=1, keepdims=True) * scale
 
-    wide_ref[0] = turned(jnp.where(valid[0], norm[0], -FAR))
-    near = wide_ref[0]
-    if lanes > 128:
-        near = jnp.concatenate([near] * (lanes // 128), axis=1)
+    def repeat(block):
+        if lanes > 128:
+            block = jnp.concatenate([block] * (lanes // 128), axis=1)
+        return block
+
+    def left_of(slot, chunk):
+        return 1 if slot == half and chunk >= cut_chunk else 0
+
+    for left in range(2):
+        wide_ref[left, 0] = turned(jnp.where(valid[left], norm[left], -FAR))
     largest = jnp.zeros((1, lanes), jnp.float32)
     for slot in range(slots):
         for chunk in range(chunks):
             cut = slice(chunk * lanes, (chunk + 1) * lanes)
+            near = repeat(wide_ref[left_of(slot, chunk), 0])
             tile = jnp.max(
                 near - (2.0 * scale) * inner_ref[slot * chunks + chunk], axis=0, keepdims=True
             )
@@ -329,54 +384,58 @@
             held.append(cover)
         covers.append(held)
 
-    for turn in range(steps):
-        wide_ref[turn] = turned(
-            jnp.where(valid[0], bound - norm[0] - covers[0][turn], -FAR)
-        )
+    for left in range(2):
+        for turn in range(steps):
+            wide_ref[left, turn] = turned(
+                jnp.where(valid[left], bound - norm[left] - covers[left][turn], -FAR)
+            )
+        wide_ref[left, steps] = turned(bound - norm[left])
     row_gain_ref[...] = jnp.zeros_like(row_gain_ref)
-    open_near = turned(bound - norm[0])
-    wide_ref[steps] = open_near
-
-    def repeat(block):
-        if lanes > 128:
-            block = jnp.concatenate([block] * (lanes // 128), axis=1)
-        return block
 
     for slot in range(slots):
         for chunk in range(chunks):
             cut = slice(chunk * lanes, (chunk + 1) * lanes)
             tile = (2.0 * scale) * inner_ref[slot * chunks + chunk] - norm[slot][:, cut]
             gained = []
+            left = left_of(slot, chunk)
             for turn in range(steps):
                 gained.append(
                     jnp.sum(
-                        jnp.maximum(tile + repeat(wide_ref[turn]), 0.0), axis=0, keepdims=True
+                        jnp.maximum(tile + repeat(wide_ref[left, turn]), 0.0),
+                        axis=0,
+                        keepdims=True,
                     )
                 )
                 if slot > 0:
                     far = jnp.where(valid[slot][:, cut], covers[slot][turn][:, cut], FAR)
-                    each = jnp.maximum(tile + repeat(wide_ref[steps]) - far, 0.0)
+                    each = jnp.maximum(tile + repeat(wide_ref[left, steps]) - far, 0.0)
                     for low in range(0, lanes, 128):
-                        row_gain_ref[turn] += each[:, low : low + 128]
+                        row_gain_ref[left, turn] += each[:, low : low + 128]
             if slot == half:
-                gained = [jnp.where(gets_half, row, 0.0) for row in gained]
+                gets = gets_second if left else gets_first
+                gained = [jnp.where(gets, row, 0.0) for row in gained]
             last = covers[0][steps][:, cut] if slot == 0 else jnp.zeros((1, lanes), jnp.float32)
             blank = jnp.zeros((8 - steps - 1, lanes), jnp.float32)
             gains_ref[chunk, slot] = jnp.concatenate([*gained, last, blank], axis=0)
-    for turn in range(steps):
-        row = jnp.sum(jnp.transpose(row_gain_ref[turn]), axis=0, keepdims=True)
-        for chunk in range(chunks):
-            gains_ref[chunk, 0, turn : turn + 1] += row[:, chunk * lanes : (chunk + 1) * lanes]
+    for left in range(2):
+        for turn in range(steps):
+            row = jnp.sum(jnp.transpose(row_gain_ref[left, turn]), axis=0, keepdims=True)
+            for chunk in range(chunks):
+                cut = slice(chunk * lanes, (chunk + 1) * lanes)
+                gains_ref[chunk, left, turn : turn + 1] += row[:, cut]
 
     for hop in range(1, members):
         share_gains(hop).start()
     final_ref[0] = gains_ref[member * sub // UNIT]
     for hop in range(1, members):
         share_gains(hop).wait_recv()
+    second = (member * sub // UNIT) // cut_chunk
     for ahead in range(members):
         summed = final_ref[ahead, 0]
         for slot in range(1, slots):
-            summed = summed + final_ref[(ahead + step * slot + members) % members, slot]
+            behind = slot if slot < half else half + second
+            holder = (ahead + step * behind + members * half) % members
+            summed = summed + final_ref[holder, slot]
         block = ring_member((place + ahead) % members)
         result_ref[:, pl.ds(pl.multiple_of(block * lanes, lanes), lanes)] = summed
 
@@ -389,9 +448,13 @@
         for hop in range(1, members):
             share_picks(f, hop).wait_send()
 
-        @pl.when(sends_half)
-        def _():
-            share(f, half).wait_send()
+        @pl.when(gives_second)
+        def _():
+            share_second(f).wait_send()
+
+        @pl.when(gives_first)
+        def _():
+            share_first(f).wait_send()
 
     for hop in range(1, members):
         share_bound(hop).wait_send()
@@ -423,14 +486,16 @@
             pltpu.VMEM((slots, capacity, 128), jnp.float32),
             pltpu.VMEM((PICK_ROWS, 128), jnp.float32),
             pltpu.VMEM((members, 8, 128), jnp.float32),
-            pltpu.VMEM((steps + 1, capacity, 128), jnp.float32),
-            pltpu.VMEM((steps, capacity, 128), jnp.float32),
+            pltpu.VMEM((2, steps + 1, capacity, 128), jnp.float32),
+            pltpu.VMEM((2, steps, capacity, 128), jnp.float32),
             pltpu.VMEM((chunks, slots, 8, lanes), jnp.float32),
             pltpu.VMEM((members, slots, 8, lanes), jnp.float32),
             dma((PARTS, owners - 1)),
             dma((PARTS, owners - 1)),
-            dma((PARTS, members // 2)),
-            dma((PARTS, members // 2)),
+            dma((PARTS, members // 2 - 1)),
+            dma((PARTS, members // 2 - 1)),
+            dma((PARTS, 2)),
+            dma((PARTS, 2)),
             dma((PARTS, members - 1)),
             dma((PARTS, members - 1)),
             dma((members - 1,)),

time: 151 us -> 140 us (0.927)
  Pallas kernels: 142 us -> 132 us
    pallas_call x1, Pallas kernels: 142 us -> 132 us  [class_gains(): pl.pallas_call(functools.partial(class_kernel, members, owners, sub, step...]
where the time goes in v2:
time: 140 us
  Pallas kernels  132 us (94%)
  other arithmetic  4.04 us (3%)
  local copies, waits for them, and re-layouts  2.86 us (2%)
    pallas_call x1, Pallas kernels, class_gains(): pl.pallas_call(functools.partial(class_kernel, members, owners, sub, step...  132 us

profile of v2, /device:TPU:24, one launch (start us, length us, event | category | flops | bytes accessed | tf_op | source)
XLA Modules:
  0.0 140.0 jit_solution(13799757170528653586)
XLA Ops:
  0.6 0.0 copy-start
  0.6 0.7 dynamic-slice_bitcast_fusion
  1.4 0.1 iota_compare_fusion
  1.5 0.1 reshape.43
  1.5 0.7 copy.12
  2.3 0.6 pad.4.pick_ref
  2.9 1.3 fusion.16
  4.2 131.8 %shard_map.68 = f32[8,512]{1,0:T(8,128)} custom-call(s32[1,256]{1,0:T(1,128)} %bitcast.5, s32[16,128]{1,0:T(8,128)} %pad.4.pick_ref, s32[1,4,32]{2,1,0:T(4,128)} %counts_ref.1, bf16[256,4096]{1,0:T(8,128)(2,1)} %sketch_ref.1), custom_call_target="tpu_custom_call" | custom-call | tf_op jit(solution)/shard_map/pallas_call | solution.py:474
  136.0 0.0 copy-done
  136.0 0.6 reduce_sum.9
  137.3 0.7 divide_bitcast_fusion
  138.0 0.6 copy.16
  138.6 0.1 lt.62
  138.7 1.3 slice_select_fusion
  (1 shorter events, 0.0 us)
Async XLA Ops:
  0.6 135.3 %copy-start = (s32[1,4,32]{2,1,0:T(4,128)S(1)}, s32[1,4,32]{2,1,0:T(4,128)}, u32[]{:S(2)}) copy-start(s32[1,4,32]{2,1,0:T(4,128)} %counts_ref.1) | copy-start | bytes 1540

commit v3 on v2

--- a/solution.py
+++ b/solution.py
@@ -10,7 +10,7 @@
 MESH = pl.DeviceIdType.MESH
 UNIT = 16
 PICK_ROWS = 16
-PARTS = 8
+PARTS = 16
 WINDOW = 2
 FAR = 1e30
 
@@ -23,6 +23,20 @@
 def ring_member(place):
     high = place // 2
     return 2 * high + (place % 2 + high) % 2
+
+
+def flip(index, mask):
+    bit = 1
+    while bit <= mask:
+        if mask & bit:
+            index = index + bit * (1 - 2 * (index // bit % 2))
+        bit *= 2
+    return index
+
+
+def bits(size):
+    assert size & (size - 1) == 0
+    return size.bit_length() - 1
 
 
 def dot_rows(left, right):
@@ -36,15 +50,19 @@
     owners,
     sub,
     steps,
-    target_ref,
+    labels_ref,
+    places_ref,
     pick_ref,
     counts_ref,
     sketch_ref,
-    result_ref,
+    gain_ref,
+    cover_ref,
+    sketch_part_ref,
     table_ref,
     out_ref,
     rows_ref,
     picks_ref,
+    place_ref,
     inner_ref,
     pick_inner_ref,
     squares_ref,
@@ -54,6 +72,7 @@
     row_gain_ref,
     gains_ref,
     final_ref,
+    s_sem,
     a_send,
     a_recv,
     b_send,
@@ -76,6 +95,7 @@
     capacity = chunks * lanes
     half = members // 2
     slots = half + 1
+    pairs = owners // 2
     window = min(WINDOW, parts - 1)
     place = ring_place(member)
     step = 1 - 2 * (owner % 2)
@@ -86,11 +106,12 @@
     gives_first = (ring + 1) % members < half
     gives_second = ring >= half
     scale = 1.0 / width
+    order = [*range(pairs // 2, pairs), *range(pairs // 2 - 1, -1, -1)]
 
     barrier = pltpu.get_barrier_semaphore()
-    for hop in range(1, owners):
+    for mask in range(1, owners):
         pl.semaphore_signal(
-            barrier, inc=1, device_id=(member, (owner + hop) % owners), device_id_type=MESH
+            barrier, inc=1, device_id=(member, flip(owner, mask)), device_id_type=MESH
         )
     for hop in range(1, members):
         pl.semaphore_signal(
@@ -100,45 +121,60 @@
             device_id_type=MESH,
         )
 
-    def dispatch(f, hop):
-        target = (owner + hop) % owners
+    def fetch(f):
+        low = pl.multiple_of(f * part, part)
+        return pltpu.make_async_copy(
+            sketch_ref.at[:, pl.ds(low, part)], sketch_part_ref.at[f], s_sem.at[f]
+        )
+
+    def dispatch(f, mask):
+        target = flip(owner, mask)
         return pltpu.make_async_remote_copy(
             src_ref=out_ref.at[f, target],
             dst_ref=rows_ref.at[0, f, :, owner],
-            send_sem=a_send.at[f, hop - 1],
-            recv_sem=a_recv.at[f, hop - 1],
+            send_sem=a_send.at[f, mask - 1],
+            recv_sem=a_recv.at[f, mask - 1],
             device_id=(member, target),
             device_id_type=MESH,
         )
 
-    def share(f, hop):
+    def dispatch_all(f):
+        for pair in order:
+            for mask in (2 * pair, 2 * pair + 1):
+                if mask:
+                    dispatch(f, mask).start()
+
+    def sources(pair):
+        return pl.ds(2 * flip(owner // 2, pair), 2)
+
+    def share(f, hop, pair):
         target = ring_member((place + step * hop + members) % members)
         return pltpu.make_async_remote_copy(
-            src_ref=rows_ref.at[0, f],
-            dst_ref=rows_ref.at[hop, f],
-            send_sem=b_send.at[f, hop - 1],
-            recv_sem=b_recv.at[f, hop - 1],
+            src_ref=rows_ref.at[0, f, :, sources(pair)],
+            dst_ref=rows_ref.at[hop, f, :, sources(pair)],
+            send_sem=b_send.at[f, hop - 1, pair],
+            recv_sem=b_recv.at[f, hop - 1, pair],
             device_id=(target, owner),
             device_id_type=MESH,
         )
 
-    def share_first(f):
+    def share_first(f, pair):
         return pltpu.make_async_remote_copy(
-            src_ref=rows_ref.at[half - 1, f, :cut_chunk],
-            dst_ref=rows_ref.at[half, f, :cut_chunk],
-            send_sem=x_send.at[f, 0],
-            recv_sem=x_recv.at[f, 0],
+            src_ref=rows_ref.at[half - 1, f, :cut_chunk, sources(pair)],
+            dst_ref=rows_ref.at[half, f, :cut_chunk, sources(pair)],
+            send_sem=x_send.at[f, 0, pair],
+            recv_sem=x_recv.at[f, 0, pair],
             device_id=(ring_member((place + step + members) % members), owner),
             device_id_type=MESH,
         )
 
-    def share_second(f):
+    def share_second(f, pair):
         target = ring_member((place + step * (half + 1) + members * half) % members)
         return pltpu.make_async_remote_copy(
-            src_ref=rows_ref.at[0, f, cut_chunk:],
-            dst_ref=rows_ref.at[half, f, cut_chunk:],
-            send_sem=x_send.at[f, 1],
-            recv_sem=x_recv.at[f, 1],
+            src_ref=rows_ref.at[0, f, cut_chunk:, sources(pair)],
+            dst_ref=rows_ref.at[half, f, cut_chunk:, sources(pair)],
+            send_sem=x_send.at[f, 1, pair],
+            recv_sem=x_recv.at[f, 1, pair],
             device_id=(target, owner),
             device_id_type=MESH,
         )
@@ -175,10 +211,10 @@
         )
 
     def prepare(f):
-        low = pl.multiple_of(f * part, part)
+        fetch(f).wait()
         block = jnp.dot(
             table_ref[...],
-            sketch_ref[:, pl.ds(low, part)],
+            sketch_part_ref[f],
             preferred_element_type=jnp.float32,
         ).astype(out_ref.dtype)
         out_ref[f] = block.reshape(out_ref.shape[1:])
@@ -217,12 +253,13 @@
             share_picks(f, hop).start()
 
     def other_part(f):
-        for hop in range(1, half):
-            share(f, hop).wait_recv()
-
-        @pl.when(gives_first)
-        def _():
-            share_first(f).start()
+        for pair in range(pairs):
+            for hop in range(1, half):
+                share(f, hop, pair).wait_recv()
+
+            @pl.when(gives_first)
+            def _(pair=pair):
+                share_first(f, pair).start()
 
         for hop in range(1, members):
             share_picks(f, hop).wait_recv()
@@ -242,73 +279,59 @@
 
         @pl.when(gets_second)
         def _():
-            share_second(f).wait_recv()
+            for pair in range(pairs):
+                share_second(f, pair).wait_recv()
             multiply(half, f, 1, cut_chunk, chunks)
             multiply_picks(half, f, picks, cut_chunk, chunks)
 
         @pl.when(gets_first)
         def _():
-            share_first(f).wait_recv()
+            for pair in range(pairs):
+                share_first(f, pair).wait_recv()
             multiply(half, f, 0, 0, cut_chunk)
             multiply_picks(half, f, picks, 0, cut_chunk)
 
+    for f in range(parts):
+        fetch(f).start()
+    label_bits, place_bits, sub_bits = bits(members), bits(members * owners * sub), bits(sub)
+    unit_bits = bits(UNIT)
+    places = places_ref[...]
+    target = (labels_ref[...] << label_bits) + (places >> place_bits)
+    target = (target << sub_bits) + (places & (sub - 1))
     table_ref[...] = (
-        lax.broadcasted_iota(jnp.int32, (2 * row_count, row_count), 0) == target_ref[...]
+        lax.broadcasted_iota(jnp.int32, (2 * row_count, row_count), 0) == target
     ).astype(table_ref.dtype)
     for f in range(window + 1):
         prepare(f)
     pl.semaphore_wait(barrier, owners + members - 2)
     for f in range(window):
-        for hop in range(1, owners):
-            dispatch(f, hop).start()
+        dispatch_all(f)
 
     inner_ref[...] = jnp.zeros_like(inner_ref)
     pick_inner_ref[...] = jnp.zeros_like(pick_inner_ref)
     squares_ref[...] = jnp.zeros_like(squares_ref)
     pick_squares_ref[...] = jnp.zeros_like(pick_squares_ref)
+    row_gain_ref[...] = jnp.zeros_like(row_gain_ref)
+
+    chosen = pick_ref[...]
+    source = (chosen & (members * owners * sub - 1)) >> sub_bits
+    offset = ((chosen >> place_bits) << sub_bits) + (chosen & (sub - 1))
+    chosen = ((offset >> unit_bits) << bits(owners)) + (source & (owners - 1))
+    chosen = (chosen << unit_bits) + (offset & (UNIT - 1)) + (source >> bits(owners)) * capacity
+    turn_row = lax.broadcasted_iota(jnp.int32, (PICK_ROWS, capacity), 0)
+    wanted = jnp.full((PICK_ROWS, capacity), -1, jnp.int32)
+    for turn in range(steps):
+        wanted = jnp.where(turn_row == turn, chosen[:, turn : turn + 1], wanted)
     pick_table = (
-        lax.broadcasted_iota(jnp.int32, (PICK_ROWS, capacity), 1) + member * capacity
-        == pick_ref[:, :1]
+        lax.broadcasted_iota(jnp.int32, (PICK_ROWS, capacity), 1) + member * capacity == wanted
     ).astype(rows_ref.dtype)
 
-    @pl.loop(0, parts)
-    def _(f):
-        for hop in range(1, owners):
-            dispatch(f, hop).wait_recv()
-
-        for hop in range(1, half):
-            share(f, hop).start()
-
-        @pl.when(gives_second)
-        def _():
-            share_second(f).start()
-
-        @pl.when(f + window < parts)
-        def _():
-            for hop in range(1, owners):
-                dispatch(f + window, hop).start()
-
-        @pl.when(f + window + 1 < parts)
-        def _():
-            prepare(f + window + 1)
-
-        own_part(f)
-
-        @pl.when(f > 0)
-        def _():
-            other_part(f - 1)
-
-    other_part(parts - 1)
-
+    lows = UNIT // sub
     lane = lax.broadcasted_iota(jnp.int32, (members * owners, lanes), 1)
     source = lax.broadcasted_iota(jnp.int32, (members * owners, lanes), 0)
     spot = lax.broadcasted_iota(jnp.int32, (1, lanes), 1) & (sub - 1)
-    lows = UNIT // sub
-    unit_bits = UNIT.bit_length() - 1
-    sub_bits = sub.bit_length() - 1
-
-    def block_row(behind):
-        block = ring_member((place - step * behind + members * half) % members)
+    for ahead in range(members):
+        block = ring_member((place + ahead) % members)
         filled = jnp.zeros((chunks, lanes), jnp.float32)
         for low in range(lows):
             spread_out = (source == block * owners + (lane >> unit_bits)) & (
@@ -319,8 +342,42 @@
                 spread_out.astype(jnp.bfloat16),
                 preferred_element_type=jnp.float32,
             )
-        row = (filled > spot.astype(jnp.float32)).astype(jnp.float32)
-        return jnp.concatenate([row[chunk : chunk + 1] for chunk in range(chunks)], axis=1)
+        place_ref[ahead] = (filled > spot.astype(jnp.float32)).astype(jnp.float32)
+    total = jnp.sum(counts_ref[...].astype(jnp.float32), axis=0)
+    total = jnp.sum(jnp.sum(total, axis=0, keepdims=True), axis=1, keepdims=True)
+
+    @pl.loop(0, parts)
+    def _(f):
+        for pair in range(pairs):
+            for mask in (2 * pair, 2 * pair + 1):
+                if mask:
+                    dispatch(f, mask).wait_recv()
+            for hop in range(1, half):
+                share(f, hop, pair).start()
+
+            @pl.when(gives_second)
+            def _(pair=pair):
+                share_second(f, pair).start()
+
+        @pl.when(f + window < parts)
+        def _():
+            dispatch_all(f + window)
+
+        @pl.when(f + window + 1 < parts)
+        def _():
+            prepare(f + window + 1)
+
+        own_part(f)
+
+        @pl.when(f > 0)
+        def _():
+            other_part(f - 1)
+
+    other_part(parts - 1)
+
+    def block_row(behind):
+        rows = place_ref[(members * half - step * behind) % members]
+        return jnp.concatenate([rows[chunk : chunk + 1] for chunk in range(chunks)], axis=1)
 
     def valid_row(slot):
         if slot < half:
@@ -360,37 +417,35 @@
             )
             tile = jnp.where(valid[slot][:, cut], tile + norm[slot][:, cut], 0.0)
             largest = jnp.maximum(largest, tile)
-    bound_ref[0] = jnp.broadcast_to(jnp.max(largest, axis=1, keepdims=True), bound_ref.shape[1:])
+    largest = jnp.max(largest, axis=1, keepdims=True)
+    bound_ref[0] = jnp.broadcast_to(largest, bound_ref.shape[1:])
     for hop in range(1, members):
         share_bound(hop).start()
-    for hop in range(1, members):
-        share_bound(hop).wait_recv()
-    bound = bound_ref[0]
-    for hop in range(1, members):
-        bound = jnp.maximum(bound, bound_ref[hop])
-    bound = bound[:1, :1]
-
-    covers = []
+
+    tops = []
     for slot in range(slots):
-        cover = jnp.zeros((1, capacity), jnp.float32)
-        held = [cover]
+        top = None
+        held = [jnp.broadcast_to(largest, (1, capacity))]
         for turn in range(steps):
-            similar = bound - (
+            apart = (
                 pick_norm[turn : turn + 1]
                 + norm[slot]
                 - (2.0 * scale) * pick_inner_ref[slot][turn : turn + 1]
             )
-            cover = jnp.maximum(cover, similar)
-            held.append(cover)
-        covers.append(held)
+            top = apart if top is None else jnp.minimum(top, apart)
+            held.append(top)
+        tops.append(held)
 
     for left in range(2):
         for turn in range(steps):
             wide_ref[left, turn] = turned(
-                jnp.where(valid[left], bound - norm[left] - covers[left][turn], -FAR)
+                jnp.where(valid[left], tops[left][turn] - norm[left], -FAR)
             )
-        wide_ref[left, steps] = turned(bound - norm[left])
-    row_gain_ref[...] = jnp.zeros_like(row_gain_ref)
+        wide_ref[left, steps] = turned(-norm[left])
+    sizes = [
+        jnp.sum(valid[left].astype(jnp.float32), axis=1, keepdims=True) for left in range(2)
+    ]
+    far_sizes = [jnp.zeros((1, 1), jnp.float32) for left in range(2)]
 
     for slot in range(slots):
         for chunk in range(chunks):
@@ -407,29 +462,47 @@
                     )
                 )
                 if slot > 0:
-                    far = jnp.where(valid[slot][:, cut], covers[slot][turn][:, cut], FAR)
-                    each = jnp.maximum(tile + repeat(wide_ref[left, steps]) - far, 0.0)
+                    far = jnp.where(valid[slot][:, cut], tops[slot][turn][:, cut], -FAR)
+                    each = jnp.maximum(tile + repeat(wide_ref[left, steps]) + far, 0.0)
                     for low in range(0, lanes, 128):
                         row_gain_ref[left, turn] += each[:, low : low + 128]
+            gained.append(
+                tops[0][steps][:, cut] if slot == 0 else jnp.zeros((1, lanes), jnp.float32)
+            )
+            gained.append(jnp.broadcast_to(largest * sizes[left], (1, lanes)))
             if slot == half:
                 gets = gets_second if left else gets_first
                 gained = [jnp.where(gets, row, 0.0) for row in gained]
-            last = covers[0][steps][:, cut] if slot == 0 else jnp.zeros((1, lanes), jnp.float32)
-            blank = jnp.zeros((8 - steps - 1, lanes), jnp.float32)
-            gains_ref[chunk, slot] = jnp.concatenate([*gained, last, blank], axis=0)
+            if slot > 0:
+                far_sizes[left] = far_sizes[left] + jnp.sum(
+                    valid[slot][:, cut].astype(jnp.float32), axis=1, keepdims=True
+                )
+            gained.append(jnp.zeros((8 - steps - 2, lanes), jnp.float32))
+            gains_ref[chunk, slot] = jnp.concatenate(gained, axis=0)
     for left in range(2):
         for turn in range(steps):
             row = jnp.sum(jnp.transpose(row_gain_ref[left, turn]), axis=0, keepdims=True)
             for chunk in range(chunks):
                 cut = slice(chunk * lanes, (chunk + 1) * lanes)
                 gains_ref[chunk, left, turn : turn + 1] += row[:, cut]
+        for chunk in range(chunks):
+            gains_ref[chunk, left, steps + 1 : steps + 2] += jnp.broadcast_to(
+                largest * far_sizes[left], (1, lanes)
+            )
 
     for hop in range(1, members):
         share_gains(hop).start()
     final_ref[0] = gains_ref[member * sub // UNIT]
     for hop in range(1, members):
+        share_bound(hop).wait_recv()
+    bound = bound_ref[0]
+    for hop in range(1, members):
+        bound = jnp.maximum(bound, bound_ref[hop])
+    bound = bound[:1, :1]
+    for hop in range(1, members):
         share_gains(hop).wait_recv()
-    second = (member * sub // UNIT) // cut_chunk
+    chunk_here = member * sub // UNIT
+    second = chunk_here // cut_chunk
     for ahead in range(members):
         summed = final_ref[ahead, 0]
         for slot in range(1, slots):
@@ -437,31 +510,41 @@
             holder = (ahead + step * behind + members * half) % members
             summed = summed + final_ref[holder, slot]
         block = ring_member((place + ahead) % members)
-        result_ref[:, pl.ds(pl.multiple_of(block * lanes, lanes), lanes)] = summed
+        here = pl.ds(pl.multiple_of(block * lanes, lanes), lanes)
+        used = place_ref[ahead, pl.ds(chunk_here, 1)]
+        for turn in range(steps):
+            row = summed[turn : turn + 1]
+            if turn == 0:
+                row = row + (total * bound - summed[steps + 1 : steps + 2])
+            gain_ref[turn, :, here] = row * used / total
+        cover_ref[:, here] = jnp.maximum(bound - summed[steps : steps + 1], 0.0) * used
 
     @pl.loop(0, parts)
     def _(f):
-        for hop in range(1, owners):
-            dispatch(f, hop).wait_send()
-        for hop in range(1, half):
-            share(f, hop).wait_send()
+        for mask in range(1, owners):
+            dispatch(f, mask).wait_send()
+        for pair in range(pairs):
+            for hop in range(1, half):
+                share(f, hop, pair).wait_send()
         for hop in range(1, members):
             share_picks(f, hop).wait_send()
 
         @pl.when(gives_second)
         def _():
-            share_second(f).wait_send()
+            for pair in range(pairs):
+                share_second(f, pair).wait_send()
 
         @pl.when(gives_first)
         def _():
-            share_first(f).wait_send()
+            for pair in range(pairs):
+                share_first(f, pair).wait_send()
 
     for hop in range(1, members):
         share_bound(hop).wait_send()
         share_gains(hop).wait_send()
 
 
-def class_gains(target, picks, counts, sketches, members, owners, sub, steps):
+def class_gains(labels, places, picks, counts, sketches, members, owners, sub, steps):
     row_count, width = sketches.shape
     chunks = members * sub // UNIT
     lanes = owners * UNIT
@@ -473,14 +556,19 @@
     dma = pltpu.SemaphoreType.DMA
     return pl.pallas_call(
         functools.partial(class_kernel, members, owners, sub, steps),
-        out_shape=jax.ShapeDtypeStruct((8, members * lanes), jnp.float32),
-        in_specs=[vmem, vmem, vmem, vmem],
-        out_specs=vmem,
+        out_shape=(
+            jax.ShapeDtypeStruct((steps, 1, members * lanes), jnp.float32),
+            jax.ShapeDtypeStruct((1, members * lanes), jnp.float32),
+        ),
+        in_specs=[vmem, vmem, vmem, vmem, pl.BlockSpec(memory_space=pl.ANY)],
+        out_specs=(vmem, vmem),
         scratch_shapes=[
+            pltpu.VMEM((PARTS, row_count, part), kind),
             pltpu.VMEM((2 * row_count, row_count), kind),
             pltpu.VMEM((PARTS, owners, chunks, UNIT, part), kind),
             pltpu.VMEM((slots, PARTS, chunks, owners, UNIT, part), kind),
             pltpu.VMEM((members, PARTS, PICK_ROWS, part), kind),
+            pltpu.VMEM((members, chunks, lanes), jnp.float32),
             pltpu.VMEM((slots * chunks, capacity, lanes), jnp.float32),
             pltpu.VMEM((slots, PICK_ROWS, capacity), jnp.float32),
             pltpu.VMEM((slots, capacity, 128), jnp.float32),
@@ -490,12 +578,13 @@
             pltpu.VMEM((2, steps, capacity, 128), jnp.float32),
             pltpu.VMEM((chunks, slots, 8, lanes), jnp.float32),
             pltpu.VMEM((members, slots, 8, lanes), jnp.float32),
+            dma((PARTS,)),
             dma((PARTS, owners - 1)),
             dma((PARTS, owners - 1)),
-            dma((PARTS, members // 2 - 1)),
-            dma((PARTS, members // 2 - 1)),
-            dma((PARTS, 2)),
-            dma((PARTS, 2)),
+            dma((PARTS, members // 2 - 1, owners // 2)),
+            dma((PARTS, members // 2 - 1, owners // 2)),
+            dma((PARTS, 2, owners // 2)),
+            dma((PARTS, 2, owners // 2)),
             dma((PARTS, members - 1)),
             dma((PARTS, members - 1)),
             dma((members - 1,)),
@@ -506,7 +595,7 @@
         compiler_params=pltpu.CompilerParams(
             collective_id=0, has_side_effects=True, vmem_limit_bytes=60 * 1024 * 1024
         ),
-    )(target, picks, counts, sketches)
+    )(labels, places, picks, counts, sketches)
 
 
 def body(sketches, labels, places, counts, chosen):
@@ -521,29 +610,25 @@
     member = lax.axis_index("dp")
     steps = chosen.shape[0]
 
-    target = (labels * members + places // capacity) * sub + places % sub
-    source = chosen % capacity // sub
-    offset = chosen // capacity * sub + chosen % sub
-    pick = (offset // UNIT * owners + source % owners) * UNIT + offset % UNIT
-    pick = jnp.pad(
-        source // owners * capacity + pick, ((0, PICK_ROWS - steps), (0, 127)), constant_values=-1
+    filled = jnp.transpose(counts[0].reshape(chunks, lows, devices), (1, 0, 2))
+    gain_scores, coverage = class_gains(
+        labels.reshape(1, row_count),
+        places.reshape(1, row_count),
+        chosen.reshape(1, steps),
+        filled,
+        sketches,
+        members,
+        owners,
+        sub,
+        steps,
     )
-    class_counts = counts[0]
-    filled = jnp.transpose(class_counts.reshape(chunks, lows, devices), (1, 0, 2))
-
-    result = class_gains(
-        target.reshape(1, row_count), pick, filled, sketches, members, owners, sub, steps
-    )
-    total = jnp.sum(class_counts).astype(jnp.float32)
     if lows > 1:
-        result = lax.dynamic_index_in_dim(
-            result.reshape(8, members * owners, lows, sub), member % lows, 2, False
-        ).reshape(8, capacity)
-    mine = lax.dynamic_index_in_dim(class_counts, member, 0, False)
-    spot = lax.broadcasted_iota(jnp.int32, (devices, sub), 1)
-    place_valid = (spot < mine[:, None]).reshape(capacity).astype(jnp.float32)
-    gain_scores = (result[:steps] * place_valid[None, :] / total)[:, None, :]
-    coverage = (result[steps] * place_valid)[None, :]
+        gain_scores = lax.dynamic_index_in_dim(
+            gain_scores.reshape(steps, 1, members * owners, lows, sub), member % lows, 3, False
+        ).reshape(steps, 1, capacity)
+        coverage = lax.dynamic_index_in_dim(
+            coverage.reshape(1, members * owners, lows, sub), member % lows, 2, False
+        ).reshape(1, capacity)
     return (gain_scores, coverage)
 
 

time: 140 us -> 127 us (0.907)
  the two profiles are of different devices: /device:TPU:24 before, /device:TPU:0 now
where the time goes in v3:
time: 127 us
  Pallas kernels  124 us (98%)
  local copies, waits for them, and re-layouts  2.52 us (2%)
    pallas_call x1, Pallas kernels, class_gains(): pl.pallas_call(functools.partial(class_kernel, members, owners, sub, step...  124 us

profile of v3, /device:TPU:0, one launch (start us, length us, event | category | flops | bytes accessed | tf_op | source)
XLA Modules:
  0.0 126.9 jit_solution(15023499802031549235)
XLA Ops:
  0.6 123.8 %shard_map.68 = (f32[3,1,512]{2,1,0:T(1,128)}, f32[1,512]{1,0:T(1,128)}) custom-call(s32[1,256]{1,0:T(1,128)} %bitcast.3, s32[1,256]{1,0:T(1,128)} %bitcast.4, s32[1,3]{1,0:T(1,128)} %bitcast.5, s32[1,4,32]{2,1,0:T(4,128)} %counts_ref.1, bf16[256,4096]{1,0:T(8,128)(2,1)} %sketch_ref.1), custom_call_target="tpu_custom_call" | custom-call | tf_op jit(solution)/shard_map/pallas_call | solution.py:557
  124.4 1.3 %copy.9 = f32[3,1,512]{2,1,0:T(1,128)} copy(f32[3,1,512]{2,1,0:T(1,128)} %get-tuple-element.4) | data formatting | bytes 12288
  125.7 1.2 copy.10

commit v4 on v3

--- a/solution.py
+++ b/solution.py
@@ -106,7 +106,6 @@
     gives_first = (ring + 1) % members < half
     gives_second = ring >= half
     scale = 1.0 / width
-    order = [*range(pairs // 2, pairs), *range(pairs // 2 - 1, -1, -1)]
 
     barrier = pltpu.get_barrier_semaphore()
     for mask in range(1, owners):
@@ -139,7 +138,7 @@
         )
 
     def dispatch_all(f):
-        for pair in order:
+        for pair in range(pairs - 1, -1, -1):
             for mask in (2 * pair, 2 * pair + 1):
                 if mask:
                     dispatch(f, mask).start()
@@ -165,6 +164,16 @@
             send_sem=x_send.at[f, 0, pair],
             recv_sem=x_recv.at[f, 0, pair],
             device_id=(ring_member((place + step + members) % members), owner),
+            device_id_type=MESH,
+        )
+
+    def share_direct(f, pair):
+        return pltpu.make_async_remote_copy(
+            src_ref=rows_ref.at[0, f, :cut_chunk, sources(pair)],
+            dst_ref=rows_ref.at[half, f, :cut_chunk, sources(pair)],
+            send_sem=x_send.at[f, 0, pair],
+            recv_sem=x_recv.at[f, 0, pair],
+            device_id=(ring_member((place + half) % members), owner),
             device_id_type=MESH,
         )
 
@@ -252,14 +261,16 @@
         for hop in range(1, members):
             share_picks(f, hop).start()
 
-    def other_part(f):
+    def other_part(f, forward=True):
         for pair in range(pairs):
             for hop in range(1, half):
                 share(f, hop, pair).wait_recv()
 
-            @pl.when(gives_first)
-            def _(pair=pair):
-                share_first(f, pair).start()
+            if forward:
+
+                @pl.when(gives_first)
+                def _(pair=pair):
+                    share_first(f, pair).start()
 
         for hop in range(1, members):
             share_picks(f, hop).wait_recv()
@@ -359,6 +370,10 @@
             def _(pair=pair):
                 share_second(f, pair).start()
 
+            @pl.when(gives_second & (f == parts - 1))
+            def _(pair=pair):
+                share_direct(f, pair).start()
+
         @pl.when(f + window < parts)
         def _():
             dispatch_all(f + window)
@@ -373,7 +388,7 @@
         def _():
             other_part(f - 1)
 
-    other_part(parts - 1)
+    other_part(parts - 1, forward=False)
 
     def block_row(behind):
         rows = place_ref[(members * half - step * behind) % members]
@@ -405,43 +420,44 @@
     def left_of(slot, chunk):
         return 1 if slot == half and chunk >= cut_chunk else 0
 
-    for left in range(2):
-        wide_ref[left, 0] = turned(jnp.where(valid[left], norm[left], -FAR))
-    largest = jnp.zeros((1, lanes), jnp.float32)
-    for slot in range(slots):
-        for chunk in range(chunks):
-            cut = slice(chunk * lanes, (chunk + 1) * lanes)
-            near = repeat(wide_ref[left_of(slot, chunk), 0])
-            tile = jnp.max(
-                near - (2.0 * scale) * inner_ref[slot * chunks + chunk], axis=0, keepdims=True
-            )
-            tile = jnp.where(valid[slot][:, cut], tile + norm[slot][:, cut], 0.0)
-            largest = jnp.maximum(largest, tile)
-    largest = jnp.max(largest, axis=1, keepdims=True)
-    bound_ref[0] = jnp.broadcast_to(largest, bound_ref.shape[1:])
-    for hop in range(1, members):
-        share_bound(hop).start()
-
     tops = []
     for slot in range(slots):
-        top = None
-        held = [jnp.broadcast_to(largest, (1, capacity))]
+        held = []
         for turn in range(steps):
             apart = (
                 pick_norm[turn : turn + 1]
                 + norm[slot]
                 - (2.0 * scale) * pick_inner_ref[slot][turn : turn + 1]
             )
-            top = apart if top is None else jnp.minimum(top, apart)
-            held.append(top)
+            held.append(jnp.minimum(held[-1], apart) if held else apart)
         tops.append(held)
 
     for left in range(2):
-        for turn in range(steps):
+        closed = turned(jnp.where(valid[left], -norm[left], -FAR))
+        wide_ref[left, steps] = closed
+        wide_ref[left, 0] = jnp.where(closed > -0.5 * FAR, -closed, -FAR)
+        for turn in range(1, steps):
             wide_ref[left, turn] = turned(
-                jnp.where(valid[left], tops[left][turn] - norm[left], -FAR)
+                jnp.where(valid[left], tops[left][turn - 1] - norm[left], -FAR)
             )
-        wide_ref[left, steps] = turned(-norm[left])
+
+    largest = jnp.zeros((1, lanes), jnp.float32)
+    for slot in range(slots):
+        for chunk in range(chunks):
+            cut = slice(chunk * lanes, (chunk + 1) * lanes)
+            near = repeat(wide_ref[left_of(slot, chunk), 0])
+            there = jnp.where(valid[slot][:, cut], norm[slot][:, cut], FAR)
+            tile = (2.0 * scale) * inner_ref[slot * chunks + chunk] - there
+            inner_ref[slot * chunks + chunk] = tile
+            tile = jnp.max(near - tile, axis=0, keepdims=True)
+            largest = jnp.maximum(largest, jnp.where(valid[slot][:, cut], tile, 0.0))
+    largest = jnp.max(largest, axis=1, keepdims=True)
+    bound_ref[0] = jnp.broadcast_to(largest, bound_ref.shape[1:])
+    for hop in range(1, members):
+        share_bound(hop).start()
+    for left in range(2):
+        wide_ref[left, 0] = wide_ref[left, steps] + largest
+
     sizes = [
         jnp.sum(valid[left].astype(jnp.float32), axis=1, keepdims=True) for left in range(2)
     ]
@@ -450,24 +466,21 @@
     for slot in range(slots):
         for chunk in range(chunks):
             cut = slice(chunk * lanes, (chunk + 1) * lanes)
-            tile = (2.0 * scale) * inner_ref[slot * chunks + chunk] - norm[slot][:, cut]
+            tile = inner_ref[slot * chunks + chunk]
             gained = []
             left = left_of(slot, chunk)
+            if slot > 0:
+                closed = tile + repeat(wide_ref[left, steps])
             for turn in range(steps):
-                gained.append(
-                    jnp.sum(
-                        jnp.maximum(tile + repeat(wide_ref[left, turn]), 0.0),
-                        axis=0,
-                        keepdims=True,
-                    )
-                )
+                each = jnp.maximum(tile + repeat(wide_ref[left, turn]), 0.0)
+                gained.append(jnp.sum(each, axis=0, keepdims=True))
                 if slot > 0:
-                    far = jnp.where(valid[slot][:, cut], tops[slot][turn][:, cut], -FAR)
-                    each = jnp.maximum(tile + repeat(wide_ref[left, steps]) + far, 0.0)
+                    if turn > 0:
+                        each = jnp.maximum(closed + tops[slot][turn - 1][:, cut], 0.0)
                     for low in range(0, lanes, 128):
                         row_gain_ref[left, turn] += each[:, low : low + 128]
             gained.append(
-                tops[0][steps][:, cut] if slot == 0 else jnp.zeros((1, lanes), jnp.float32)
+                tops[0][steps - 1][:, cut] if slot == 0 else jnp.zeros((1, lanes), jnp.float32)
             )
             gained.append(jnp.broadcast_to(largest * sizes[left], (1, lanes)))
             if slot == half:
@@ -493,6 +506,32 @@
     for hop in range(1, members):
         share_gains(hop).start()
     final_ref[0] = gains_ref[member * sub // UNIT]
+
+    @pl.loop(0, parts)
+    def _(f):
+        for mask in range(1, owners):
+            dispatch(f, mask).wait_send()
+        for pair in range(pairs):
+            for hop in range(1, half):
+                share(f, hop, pair).wait_send()
+        for hop in range(1, members):
+            share_picks(f, hop).wait_send()
+
+        @pl.when(gives_second)
+        def _():
+            for pair in range(pairs):
+                share_second(f, pair).wait_send()
+
+        @pl.when(gives_second & (f == parts - 1))
+        def _():
+            for pair in range(pairs):
+                share_direct(f, pair).wait_send()
+
+        @pl.when(gives_first & (f < parts - 1))
+        def _():
+            for pair in range(pairs):
+                share_first(f, pair).wait_send()
+
     for hop in range(1, members):
         share_bound(hop).wait_recv()
     bound = bound_ref[0]
@@ -518,26 +557,6 @@
                 row = row + (total * bound - summed[steps + 1 : steps + 2])
             gain_ref[turn, :, here] = row * used / total
         cover_ref[:, here] = jnp.maximum(bound - summed[steps : steps + 1], 0.0) * used
-
-    @pl.loop(0, parts)
-    def _(f):
-        for mask in range(1, owners):
-            dispatch(f, mask).wait_send()
-        for pair in range(pairs):
-            for hop in range(1, half):
-                share(f, hop, pair).wait_send()
-        for hop in range(1, members):
-            share_picks(f, hop).wait_send()
-
-        @pl.when(gives_second)
-        def _():
-            for pair in range(pairs):
-                share_second(f, pair).wait_send()
-
-        @pl.when(gives_first)
-        def _():
-            for pair in range(pairs):
-                share_first(f, pair).wait_send()
 
     for hop in range(1, members):
         share_bound(hop).wait_send()

time: 127 us -> 124 us (0.976)
  the two profiles are of different devices: /device:TPU:0 before, /device:TPU:24 now
where the time goes in v4:
time: 124 us; the launch traced here: 123 us
  Pallas kernels  120 us (97%)
  local copies, waits for them, and re-layouts  2.52 us (2%)
    pallas_call x1, Pallas kernels, class_gains(): pl.pallas_call(functools.partial(class_kernel, members, owners, sub, step...  120 us
    unnamed x2, local copies, waits for them, and re-layouts  2.52 us

profile of v4, /device:TPU:24, one launch (start us, length us, event | category | flops | bytes accessed | tf_op | source)
XLA Modules:
  0.0 123.2 jit_solution(10717066711222125447)
XLA Ops:
  0.6 120.1 %shard_map.68 = (f32[3,1,512]{2,1,0:T(1,128)}, f32[1,512]{1,0:T(1,128)}) custom-call(s32[1,256]{1,0:T(1,128)} %bitcast.3, s32[1,256]{1,0:T(1,128)} %bitcast.4, s32[1,3]{1,0:T(1,128)} %bitcast.5, s32[1,4,32]{2,1,0:T(4,128)} %counts_ref.1, bf16[256,4096]{1,0:T(8,128)(2,1)} %sketch_ref.1), custom_call_target="tpu_custom_call" | custom-call | tf_op jit(solution)/shard_map/pallas_call | solution.py:576
  120.7 1.3 %copy.9 = f32[3,1,512]{2,1,0:T(1,128)} copy(f32[3,1,512]{2,1,0:T(1,128)} %get-tuple-element.4) | data formatting | bytes 12288
  122.0 1.2 copy.10

commit v5 on v4

--- a/solution.py
+++ b/solution.py
@@ -612,7 +612,7 @@
             dma((members - 1,)),
         ],
         compiler_params=pltpu.CompilerParams(
-            collective_id=0, has_side_effects=True, vmem_limit_bytes=60 * 1024 * 1024
+            collective_id=0, has_side_effects=True, vmem_limit_bytes=53 * 1024 * 1024
         ),
     )(labels, places, picks, counts, sketches)
 

time: 124 us -> 123 us (level)
  local copies, waits for them, and re-layouts: 2.52 us -> 3.86 us
    pallas_call x1, Pallas kernels: 120 us -> 119 us  [class_gains(): pl.pallas_call(functools.partial(class_kernel, members, owners, sub, step...]
    unnamed x2 -> x10, local copies, waits for them, and re-layouts: 2.52 us -> 3.86 us
where the time goes in v5:
time: 123 us
  Pallas kernels  119 us (97%)
  local copies, waits for them, and re-layouts  3.86 us (3%)
    pallas_call x1, Pallas kernels, class_gains(): pl.pallas_call(functools.partial(class_kernel, members, owners, sub, step...  119 us
    unnamed x10, local copies, waits for them, and re-layouts  3.86 us

profile of v5, /device:TPU:24, one launch (start us, length us, event | category | flops | bytes accessed | tf_op | source)
XLA Modules:
  0.0 123.0 jit_solution(17695873322411695946)
XLA Ops:
  0.6 0.0 copy-start
  0.6 0.7 copy-done
  1.3 0.0 copy-start.1
  1.3 0.7 copy-done.1
  2.0 0.0 copy-start.2
  2.0 0.7 copy-done.2
  2.7 0.0 copy-start.3
  2.7 0.7 copy-done.3
  3.3 118.5 %shard_map.68 = (f32[3,1,512]{2,1,0:T(1,128)S(1)}, f32[1,512]{1,0:T(1,128)S(1)}) custom-call(s32[1,256]{1,0:T(1,128)S(1)} %bitcast.3, s32[1,256]{1,0:T(1,128)S(1)} %bitcast.4, s32[1,3]{1,0:T(1,128)S(1)} %bitcast.5, s32[1,4,32]{2,1,0:T(4,128)S(1)} %copy-done, bf16[256,4096]{1,0:T(8,128)(2,1)} %sketch_ref.1), custom_call_target="tpu_custom_call" | custom-call | tf_op jit(solution)/shard_map/pallas_call | solution.py:576
  121.9 0.6 copy.9
  122.5 0.6 copy.10
Async XLA Ops:
  0.6 0.7 copy-start
  1.3 0.7 copy-start.1
  2.0 0.7 copy-start.2
  2.7 0.7 copy-start.3
